TPU v7x, 32 devices: a whole 2x2x4 slice. The times are simulated.
32 devices in a mesh: fsdp: 8 (over y, x, core), seq: 4 (over z).
Axes of the slice: x: 2, y: 2, z: 4, core: 2. Of those that a mesh axis runs over, the one named last changes fastest.
Arguments:
- layer_input: bfloat16 [8, 512, 4096], P('fsdp', 'seq'), may hold values from -6 to 6
- dt_weight: bfloat16 [4096, 64], P('fsdp'), may hold values from -0.09375 to 0.09375
- dt_bias: float32 [64], replicated, may hold values from -2 to -0.5
- decay_rate: float32 [64], replicated, may hold values from 0.0005 to 0.25
- ssm_input: bfloat16 [8, 512, 2048], P('fsdp', 'seq'), may hold values from -6 to 6
- in_basis: bfloat16 [8, 512, 512], P('fsdp', 'seq'), may hold values from -0.59765625 to 0.59765625
- out_basis: bfloat16 [8, 512, 512], P('fsdp', 'seq'), may hold values from -0.59765625 to 0.59765625
- out_cotangent: bfloat16 [8, 512, 2048], P('fsdp', 'seq'), may hold values from -6 to 6
Outputs:
- grad_input: bfloat16 [8, 512, 2048], P('fsdp', 'seq')
- grad_in_basis: bfloat16 [8, 512, 512], P('fsdp', 'seq')
- grad_out_basis: bfloat16 [8, 512, 512], P('fsdp', 'seq')
- grad_dt_weight: float32 [4096, 64], P('fsdp')
All inputs are finite; a program needn't handle non-finite values.
Results may differ from a plain program's by a relative error of at most 0.011.
Values may be sent and summed in bfloat16 or wider, within the bound.
A program may use at most 64 MiB of HBM per device.

v0:
```python
import jax
import jax.numpy as jnp
from jax import lax
from jax.sharding import PartitionSpec as P

STATE = 128


HIGH = lax.Precision.HIGHEST


def entering(value, axis, combine, identity):
    devices, position = (lax.axis_size(axis), lax.axis_index(axis))
    everything = jax.tree.map(
        lambda part, kind: lax.all_gather(part.astype(kind), axis),
        value,
        (jnp.bfloat16, jnp.bfloat16),
    )
    start = jax.tree.map(
        lambda part, zero: jnp.broadcast_to(jnp.asarray(zero, part.dtype), part.shape),
        value,
        identity,
    )

    def entering_step(k, before):
        reached = k < position
        new = combine(
            before, jax.tree.map(lambda part, own: part[k].astype(own.dtype), everything, value)
        )
        return jax.tree.map(lambda a, b: jnp.where(reached, a, b), new, before)

    return lax.fori_loop(0, devices, entering_step, start)


def prefix(value, axis, join, neutral):
    count, mine = (lax.axis_size(axis), lax.axis_index(axis))
    pieces = jax.tree.map(lambda part: lax.all_gather(part, axis), value)
    pieces = jax.tree.map(lambda part: part[::-1], pieces)
    mine = count - 1 - mine
    subtotal = jax.tree.map(
        lambda part, zero: jnp.full_like(part, 0) + jnp.asarray(zero, part.dtype), value, neutral
    )

    def prefix_step(position, subtotal):
        longer = join(subtotal, jax.tree.map(lambda part: part[position], pieces))
        return jax.tree.map(lambda new, old: jnp.where(position < mine, new, old), longer, subtotal)

    return lax.fori_loop(0, count - 1, prefix_step, subtotal)


def compose(earlier, later):
    decay_e, value_e = earlier
    decay_l, value_l = later
    return (decay_l * decay_e, value_l + decay_l[:, None, None] * value_e)


def body(
    layer_input, dt_weight, dt_bias, decay_rate, ssm_input, in_basis, out_basis, out_cotangent
):
    tokens = layer_input[0]
    length = tokens.shape[0]
    heads = dt_weight.shape[1]
    groups = in_basis.shape[2] // STATE
    per_group = heads // groups
    head_size = ssm_input.shape[2] // heads
    columns = tokens
    raw = (
        jnp.dot(
            columns,
            lax.all_gather(dt_weight, "fsdp", axis=0, tiled=True),
            preferred_element_type=jnp.float32,
        )
        + dt_bias
    )
    step_size = jax.nn.softplus(raw)
    rate_grid = decay_rate.reshape(groups, per_group)
    step_grid = step_size.reshape(length, groups, per_group)
    cumulative = jnp.cumsum(-decay_rate * step_size, axis=0).reshape(length, groups, per_group)
    final = cumulative[-1]
    tail = jnp.exp(final[None] - cumulative)
    leading = jnp.exp(cumulative)
    inputs_half = ssm_input[0].reshape(length, groups, per_group, head_size)
    upstream_half = out_cotangent[0].reshape(length, groups, per_group, head_size)
    bin_half = in_basis[0].reshape(length, groups, STATE)
    bout_half = out_basis[0].reshape(length, groups, STATE)
    inputs = inputs_half.astype(jnp.float32)
    upstream = upstream_half.astype(jnp.float32)
    basis_in = bin_half.astype(jnp.float32)
    basis_out = bout_half.astype(jnp.float32)
    position = jnp.arange(length)
    lower = position[:, None] >= position[None, :]
    cum_rows = cumulative.transpose(1, 2, 0)
    spread = cum_rows[:, :, :, None] - cum_rows[:, :, None, :]
    decay_mat = jnp.where(lower, jnp.exp(jnp.where(lower, spread, 0.0)), 0.0)
    intersection = jnp.einsum(
        "tgn,sgn->gts", bout_half, bin_half, preferred_element_type=jnp.float32
    )
    weighted = decay_mat * intersection[:, None]
    step_cols = step_grid.transpose(1, 2, 0)[:, :, None, :]
    local_state = jnp.einsum(
        "sgk,sgkp,sgn->gkpn", tail * step_grid, inputs, basis_in, precision=HIGH
    )
    local_grad = jnp.einsum("tgk,tgkp,tgn->gkpn", leading, upstream, basis_out, precision=HIGH)
    block_decay = jnp.exp(final).reshape(heads)
    flat_shape = (heads, head_size, STATE)
    grid_shape = (groups, per_group, head_size, STATE)
    identity = (jnp.ones((heads,), jnp.float32), jnp.zeros(flat_shape, jnp.float32))
    entry = entering((block_decay, local_state.reshape(flat_shape)), "seq", compose, identity)[
        1
    ].reshape(grid_shape)
    later = prefix((block_decay, local_grad.reshape(flat_shape)), "seq", compose, identity)[
        1
    ].reshape(grid_shape)
    pair = jnp.einsum(
        "tgkp,sgkp->gkts", upstream_half, inputs_half, preferred_element_type=jnp.float32
    )
    through = jnp.einsum("gkts,tgkp->sgkp", weighted, upstream, precision=HIGH)
    carried = jnp.einsum("sgn,gkpn->sgkp", basis_in, later, precision=HIGH)
    inner_x = through + tail[..., None] * carried
    grad_x = step_grid[..., None] * inner_x
    direct = jnp.sum(inputs * inner_x, axis=-1)
    scaled = decay_mat * pair * step_cols
    joint = jnp.sum(scaled, axis=1)
    moment = scaled * intersection[:, None]
    change = (jnp.sum(moment, axis=-1) - jnp.sum(moment, axis=-2)).transpose(2, 0, 1)
    grad_b = jnp.einsum("gts,tgn->sgn", joint, basis_out, precision=HIGH)
    grad_b = grad_b + jnp.einsum(
        "sgk,sgkp,gkpn->sgn", step_grid * tail, inputs, later, precision=HIGH
    )
    state_read = jnp.einsum("tgkp,gkpn->tgkn", upstream, entry, precision=HIGH)
    grad_c = jnp.einsum("gts,sgn->tgn", joint, basis_in, precision=HIGH)
    grad_c = grad_c + jnp.einsum("tgk,tgkn->tgn", leading, state_read, precision=HIGH)
    entry_term = leading * jnp.sum(state_read * basis_out[:, :, None, :], axis=-1)
    exit_term = tail * step_grid * jnp.sum(inputs * carried, axis=-1)
    closing = jnp.exp(final) * jnp.sum(later * entry, axis=(2, 3)) + jnp.sum(exit_term, axis=0)
    grad_cum = change + entry_term - exit_term
    grad_log = jnp.cumsum(grad_cum[::-1], axis=0)[::-1] + closing[None]
    grad_step = direct - rate_grid[None] * grad_log
    grad_raw = grad_step.reshape(length, heads) * jax.nn.sigmoid(raw)
    columns = tokens.astype(jnp.float32)
    partial_rows = lax.psum_scatter(
        jnp.dot(columns.T, grad_raw, precision=HIGH), "fsdp", scatter_dimension=0, tiled=True
    )
    grad_weight = lax.psum(partial_rows, "seq")
    out_x = grad_x.reshape(1, length, heads * head_size).astype(jnp.bfloat16)
    out_b = grad_b.reshape(1, length, groups * STATE).astype(jnp.bfloat16)
    out_c = grad_c.reshape(1, length, groups * STATE).astype(jnp.bfloat16)
    return (out_x, out_b, out_c, grad_weight)


def solution(mesh):
    placed = (
        P("fsdp", "seq", None),
        P("fsdp", None),
        P(),
        P(),
        P("fsdp", "seq", None),
        P("fsdp", "seq", None),
        P("fsdp", "seq", None),
        P("fsdp", "seq", None),
    )
    return jax.shard_map(
        body,
        mesh=mesh,
        in_specs=placed,
        out_specs=(
            P("fsdp", "seq", None),
            P("fsdp", "seq", None),
            P("fsdp", "seq", None),
            P("fsdp", None),
        ),
        check_vma=False,
    )
```

profile of v0, /device:TPU:0, one launch (start us, length us, event | category | flops | bytes accessed | tf_op | source)
XLA Modules:
  0.0 256.8 jit_solution(15940278393139724668)
XLA Ops:
  7.2 11.8 %all_gather.17 = bf16[4096,64]{0,1:T(8,128)(2,1)S(1)} all-gather(bf16[512,64]{0,1:T(8,128)(2,1)} %param.13), channel_id=1, replica_groups=mesh['fsdp'=8,'seq'=4] {'fsdp'}, dimensions={0}, use_global_device_ids=true | all-gather | bytes 589824 | tf_op jit(solution)/shard_map/all_gather | solution.py:70
  19.0 0.7 neg.11
  19.7 1.8 compare_select_fusion
  22.4 0.9 reshape_squeeze.13
  23.3 1.3 copy.82
  24.7 0.8 fusion.38
  25.5 1.4 convolution_convert_fusion
  27.3 1.6 fusion.26
  29.4 0.7 mul.166
  30.1 11.6 %all-gather = f32[4,1,64]{2,1,0:T(1,128)S(1)} all-gather(f32[1,1,64]{2,1,0:T(1,128)} %get-tuple-element.277), channel_id=1, replica_groups=mesh['fsdp'=8,'seq'=4] {'seq'}, dimensions={0}, use_global_device_ids=true | all-gather | bytes 1280 | tf_op jit(solution)/shard_map/all_gather | solution.py:37
  42.4 8.4 %all-gather.1 = bf16[4,1,64]{2,1,0:T(2,128)(2,1)S(1)} all-gather(bf16[1,1,64]{2,1,0:T(2,128)(2,1)} %get-tuple-element.278), channel_id=1, replica_groups=mesh['fsdp'=8,'seq'=4] {'seq'}, dimensions={0}, use_global_device_ids=true | all-gather | bytes 640 | tf_op jit(solution)/shard_map/all_gather | solution.py:15
  51.3 0.7 convert_element_type.107
  53.1 5.1 %multiply_reduce_fusion = (f32[4,16,128]{2,1,0:T(8,128)}, f32[4,16,128]{2,1,0:T(8,128)}, f32[4,128,128]{2,1,0:T(8,128)}) fusion(f32[4,128,128]{2,1,0:T(8,128)S(1)} %fusion.40, f32[4,16,128]{2,1,0:T(8,128)} %bitcast.131, bf16[128,4,16,32]{0,3,2,1:T(8,128)(2,1)} %bitcast.120, bf16[128,4,16,32]{0,3,2,1:T(8,128)(2,1)} %bitcast.112, ...), kind=kOutput, calls=%fused_computation.15 | convolution fusion | flops 76464128 | bytes 1720320 | tf_op jit(solution)/shard_map/tgkp,sgkp->gkts/dot_general | solution.py:114
  58.2 14.8 %all-gather.7.cloned.1.call-done = bf16[4,64,32,128]{3,2,1,0:T(8,128)(2,1)} async-done(((bf16[1,64,32,128]{3,2,1,0:T(8,128)(2,1)}), bf16[4,64,32,128]{3,2,1,0:T(8,128)(2,1)}) %all-gather.7.cloned.1.call-update) | async-done | bytes 2097168 | tf_op jit(solution)/shard_map/all_gather | solution.py:15
  73.0 8.2 %while.29 = (s32[]{:T(128)}, f32[64,32,128]{2,1,0:T(8,128)S(1)}, s32[]{:T(128)}, bf16[4,64,32,128]{3,2,1,0:T(8,128)(2,1)}, bf16[4,64]{1,0:T(4,128)(2,1)}, /*index=5*/s32[]{:T(128)}, s32[]{:T(128)}) while((s32[]{:T(128)}, f32[64,32,128]{2,1,0:T(8,128)S(1)}, s32[]{:T(128)}, bf16[4,64,32,128]{3,2,1,0:T(8,128)(2,1)}, ...), condition=%wide.region_5.6_spmd.clone, body=%wide.region_4.5_spmd.clone.sunk | while | flops 1310788 | bytes 2622185 | solution.py:32
  73.0 0.7 bitcast_convert_fusion.2
  73.7 1.4 fusion.60
  75.1 0.7 bitcast_convert_fusion.2
  75.8 1.4 fusion.60
  77.1 0.7 bitcast_convert_fusion.2
  77.8 1.4 fusion.60
  79.2 0.7 bitcast_convert_fusion.2
  79.9 1.4 fusion.60
  81.3 5.4 %fusion.3 = (f32[128,4,16]{0,2,1:T(8,128)}, f32[128,4,128]{0,2,1:T(8,128)}) fusion(f32[128,4,128]{0,2,1:T(8,128)} %convert_element_type.107, f32[128,4,16]{0,2,1:T(8,128)} %copy-done.19, f32[4,16,32,128]{3,2,1,0:T(8,128)S(1)} %bitcast.110, bf16[128,4,16,32]{0,3,2,1:T(8,128)(2,1)} %bitcast.121), kind=kOutput, calls=%fused_computation.10 | convolution fusion | flops 406773760 | bytes 2162688 | tf_op jit(solution)/shard_map/tgkp,gkpn->tgkn/dot_general | solution.py:130
  86.6 67.5 %all-gather.5.cloned.1.call-done = f32[4,64,32,128]{3,2,1,0:T(8,128)} async-done(((f32[1,64,32,128]{3,2,1,0:T(8,128)}), f32[4,64,32,128]{3,2,1,0:T(8,128)}) %all-gather.5.cloned.1.call-update) | async-done | bytes 4194320 | tf_op jit(solution)/shard_map/all_gather | solution.py:37
  154.2 4.6 %rev.12 = f32[4,64,32,128]{3,2,1,0:T(8,128)} reverse(f32[4,64,32,128]{3,2,1,0:T(8,128)} %all-gather.5.cloned.1.call-done), dimensions={0} | reverse | bytes 8388608 | tf_op jit(solution)/shard_map/rev | solution.py:38
  158.8 6.6 %while.28 = (s32[]{:T(128)}, f32[64,32,128]{2,1,0:T(8,128)S(1)}, s32[]{:T(128)}, f32[4,64,32,128]{3,2,1,0:T(8,128)}, f32[4,64]{1,0:T(4,128)}, /*index=5*/s32[]{:T(128)}, s32[]{:T(128)}) while((s32[]{:T(128)}, f32[64,32,128]{2,1,0:T(8,128)S(1)}, s32[]{:T(128)}, f32[4,64,32,128]{3,2,1,0:T(8,128)}, f32[4,64]{1,0:T(4,128)}, ...), condition=%wide.region_2.3_spmd.clone, body=%wide.region_1.2_spmd.clone.sunk | while | flops 1048580 | bytes 3146601 | solution.py:48
  158.8 0.7 dynamic-slice_bitcast_fusion.2
  159.5 1.5 fusion.59
  161.0 0.7 dynamic-slice_bitcast_fusion.2
  161.6 1.5 fusion.59
  163.1 0.7 dynamic-slice_bitcast_fusion.2
  163.8 1.5 fusion.59
  165.4 1.1 multiply_reduce_fusion.2
  166.5 0.6 convolution_bitcast_fusion.1
  167.2 4.9 %fusion.23 = (f32[128,4,16]{0,2,1:T(8,128)S(1)}, f32[128,4,16]{0,2,1:T(8,128)}, bf16[128,4,16,32]{0,3,2,1:T(8,128)(2,1)}) fusion(f32[128,4,16,32]{0,3,2,1:T(8,128)S(1)} %convolution_bitcast_fusion.1, bf16[128,4,16,32]{0,3,2,1:T(8,128)(2,1)S(1)} %bitcast.113, f32[128,4,16]{0,2,1:T(8,128)S(1)} %bitcast.132, f32[128,4,16]{0,2,1:T(8,128)S(1)} %copy-done.23, ...), kind=kOutput, calls=%fused_computation.38 | convolution fusion | flops 409190400 | bytes 3063808 | tf_op jit(solution)/shard_map/gkts,tgkp->sgkp/dot_general | solution.py:117
  172.8 0.9 fusion.39
  173.6 1.0 copy.88
  174.8 0.9 multiply_subtract_fusion
  175.6 1.5 convolution_bitcast_fusion
  177.5 1.3 fusion.21
  178.8 0.8 copy.92
  179.6 1.8 fusion.18
  181.4 30.4 %reduce-scatter.2.cloned.1.call-done = f32[512,64]{0,1:T(8,128)} async-done(((f32[4096,64]{0,1:T(8,128)}), f32[512,64]{0,1:T(8,128)}) %reduce-scatter.2.cloned.1.call-update) | async-done | bytes 131088 | tf_op jit(solution)/shard_map/reduce_scatter | solution.py:141
  212.2 0.8 copy.91
  212.9 2.0 copy.90
  215.0 33.7 %all-reduce.2.cloned.1.call-done = f32[512,64]{0,1:T(8,128)} async-done(((f32[512,64]{0,1:T(8,128)}), f32[512,64]{0,1:T(8,128)}) %all-reduce.2.cloned.1.call-update) | async-done | bytes 131088 | tf_op jit(solution)/shard_map/psum | solution.py:144
  248.7 1.6 copy.131
  (87 shorter events, 5.2 us)
Async XLA Ops:
  7.2 12.5 %copy-start = (bf16[1,128,4096]{2,1,0:T(8,128)(2,1)S(1)}, bf16[1,128,4096]{2,1,0:T(8,128)(2,1)}, u32[]{:S(2)}) copy-start(bf16[1,128,4096]{2,1,0:T(8,128)(2,1)} %param.12) | copy-start | bytes 3145732
  7.2 19.8 %copy-start.12 = (bf16[1,128,2048]{2,1,0:T(8,128)(2,1)S(1)}, bf16[1,128,2048]{2,1,0:T(8,128)(2,1)}, u32[]{:S(2)}) copy-start(bf16[1,128,2048]{2,1,0:T(8,128)(2,1)} %param.19) | copy-start | bytes 1572868
  7.2 20.1 %copy-start.16 = (bf16[1,128,512]{2,1,0:T(8,128)(2,1)S(1)}, bf16[1,128,512]{2,1,0:T(8,128)(2,1)}, u32[]{:S(2)}) copy-start(bf16[1,128,512]{2,1,0:T(8,128)(2,1)} %param.18) | copy-start | bytes 393220
  7.2 65.8 %all-gather.7.cloned.1.call-start = ((), (), s32[]{:S(2)}) async-start(), calls=%async_computation.2 | async-start | bytes 2621440 | tf_op jit(solution)/shard_map/all_gather | solution.py:15
  21.4 5.5 %copy-start.17 = (f32[128,64]{0,1:T(8,128)}, f32[128,64]{0,1:T(8,128)S(1)}, u32[]{:S(2)}) copy-start(f32[128,64]{0,1:T(8,128)S(1)} %get-tuple-element.281) | copy-start | bytes 98308
  22.3 4.6 %copy-start.9 = (f32[128,64]{0,1:T(8,128)}, f32[128,64]{0,1:T(8,128)S(1)}, u32[]{:S(2)}) copy-start(f32[128,64]{0,1:T(8,128)S(1)} %copy.76) | copy-start | bytes 98308
  24.7 4.4 %copy-start.1 = (bf16[1,128,2048]{1,2,0:T(8,128)(2,1)}, bf16[1,128,2048]{1,2,0:T(8,128)(2,1)S(1)}, u32[]{:S(2)}) copy-start(bf16[1,128,2048]{1,2,0:T(8,128)(2,1)S(1)} %copy.82) | copy-start | bytes 1572868
  25.4 1.5 copy-start.7
  25.5 3.8 %copy-start.19 = (f32[128,4,16]{0,2,1:T(8,128)}, f32[128,4,16]{0,2,1:T(8,128)S(1)}, u32[]{:S(2)}) copy-start(f32[128,4,16]{0,2,1:T(8,128)S(1)} %get-tuple-element.280) | copy-start | bytes 98308
  26.9 127.2 %all-gather.5.cloned.1.call-start = ((), (), s32[]{:S(2)}) async-start(), calls=%async_computation.1 | async-start | bytes 5242880 | tf_op jit(solution)/shard_map/all_gather | solution.py:37
  27.3 1.8 copy-start.4
  29.0 182.9 %reduce-scatter.2.cloned.1.call-start = ((), (), s32[]{:S(2)}) async-start(), calls=%async_computation.3 | async-start | bytes 1179648 | tf_op jit(solution)/shard_map/reduce_scatter | solution.py:141
  52.1 0.6 copy-start.24
  52.3 0.7 copy-start.14
  165.3 1.8 copy-start.2
  165.3 1.8 copy-start.5
  165.4 1.8 copy-start.10
  165.4 1.8 copy-start.15
  165.4 1.8 copy-start.18
  165.4 1.8 copy-start.23
  165.4 1.8 copy-start.25
  167.2 5.0 %copy-start.13 = (f32[128,64]{0,1:T(8,128)S(1)}, f32[128,64]{0,1:T(8,128)}, u32[]{:S(2)}) copy-start(f32[128,64]{0,1:T(8,128)} %get-tuple-element.283) | copy-start | bytes 98308
  167.2 5.2 %copy-start.26 = (f32[64]{0:T(128)S(1)}, f32[64]{0:T(128)}, u32[]{:S(2)}) copy-start(f32[64]{0:T(128)} %multiply_reduce_fusion.2) | copy-start | bytes 772
  167.2 5.3 %copy-start.8 = (f32[128,4,16]{0,2,1:T(8,128)S(1)}, f32[128,4,16]{0,2,1:T(8,128)}, u32[]{:S(2)}) copy-start(f32[128,4,16]{0,2,1:T(8,128)} %copy-done.7) | copy-start | bytes 98308
  167.2 5.3 %copy-start.11 = (f32[128,64]{0,1:T(8,128)S(1)}, f32[128,64]{0,1:T(8,128)}, u32[]{:S(2)}) copy-start(f32[128,64]{0,1:T(8,128)} %copy-done.9) | copy-start | bytes 98308
  167.2 5.3 %copy-start.20 = (f32[4,16,128]{2,1,0:T(8,128)S(1)}, f32[4,16,128]{2,1,0:T(8,128)}, u32[]{:S(2)}) copy-start(f32[4,16,128]{2,1,0:T(8,128)} %get-tuple-element.246) | copy-start | bytes 98308
  167.2 5.3 %copy-start.21 = (f32[4,16,128]{2,1,0:T(8,128)S(1)}, f32[4,16,128]{2,1,0:T(8,128)}, u32[]{:S(2)}) copy-start(f32[4,16,128]{2,1,0:T(8,128)} %get-tuple-element.247) | copy-start | bytes 98308
  167.2 5.3 %copy-start.22 = (f32[128,4,16]{0,2,1:T(8,128)S(1)}, f32[128,4,16]{0,2,1:T(8,128)}, u32[]{:S(2)}) copy-start(f32[128,4,16]{0,2,1:T(8,128)} %get-tuple-element.249) | copy-start | bytes 98308
  172.1 5.4 %copy-start.6 = (f32[4,128,128]{2,1,0:T(8,128)S(1)}, f32[4,128,128]{2,1,0:T(8,128)}, u32[]{:S(2)}) copy-start(f32[4,128,128]{2,1,0:T(8,128)} %get-tuple-element.248) | copy-start | bytes 786436
  172.1 7.5 %copy-start.3 = (bf16[1,128,2048]{1,2,0:T(8,128)(2,1)S(1)}, bf16[1,128,2048]{1,2,0:T(8,128)(2,1)}, u32[]{:S(2)}) copy-start(bf16[1,128,2048]{1,2,0:T(8,128)(2,1)} %copy-done.1) | copy-start | bytes 1572868
  177.2 71.5 %all-reduce.2.cloned.1.call-start = ((), (), s32[]{:S(2)}) async-start(), calls=%async_computation.4 | async-start | bytes 262144 | tf_op jit(solution)/shard_map/psum | solution.py:144
Sparse Core Ops, SparseCore 0:
  27.0 45.9 all-gather.6
  74.6 79.5 all-gather.4
  177.3 34.4 reduce-scatter.1
  214.0 34.6 all-reduce.1
where the time goes:
time: 258 us; the launch traced here: 257 us
  waiting for transfers between devices  147 us (57%)
  blocking collectives  31.8 us (12%)
  matrix products  26 us (10%)
  local copies, waits for them, and re-layouts  19.2 us (7%)
  other arithmetic  18.5 us (7%)
  between operations  14.3 us (6%)
    all_gather x1, waiting for transfers between devices, prefix(): pieces = jax.tree.map(lambda part: lax.all_gather(part, axis), value)  67.5 us
    psum x1, waiting for transfers between devices, body(): grad_weight = lax.psum(partial_rows, 'seq')  33.7 us
    reduce_scatter x1, waiting for transfers between devices, body(): lax.psum_scatter(jnp.dot(columns.T, grad_raw, precision=HIGH), 'fsdp', sc...  30.4 us
    all_gather x1, waiting for transfers between devices, entering(): lax.all_gather(part.astype(kind), axis)  14.8 us
    all_gather x1, blocking collectives, body(): lax.all_gather(dt_weight, 'fsdp', axis=0, tiled=True)  11.8 us
    all_gather x1, blocking collectives, prefix(): pieces = jax.tree.map(lambda part: lax.all_gather(part, axis), value)  11.6 us
    all_gather x1, blocking collectives, entering(): lax.all_gather(part.astype(kind), axis)  8.39 us
    unnamed x61, local copies, waits for them, and re-layouts  8.16 us
  transfers between devices with their start and end apart: 4, of which 4 were waited for; matrix products, arithmetic and copies ran while one was open for 12% of the time, Pallas kernels for 0%

commit v1 on v0

v1 whole, which is shorter than its diff:
```python
import functools

import jax
import jax.numpy as jnp
from jax import lax
from jax.experimental import pallas as pl
from jax.experimental.pallas import tpu as pltpu
from jax.sharding import PartitionSpec as P

STATE = 128
F32 = jnp.float32
BF16 = jnp.bfloat16
MESH = pl.DeviceIdType.MESH
HIGH = lax.Precision.HIGHEST


def dot(a, b, ca=1, cb=0, precision=None):
    return lax.dot_general(
        a, b, (((ca,), (cb,)), ((), ())), precision=precision, preferred_element_type=F32
    )


def halves(value, axis):
    high = value.astype(BF16)
    low = (value - high.astype(F32)).astype(BF16)
    return jnp.concatenate([high, low], axis=axis)


def iota(shape, dim):
    return lax.broadcasted_iota(jnp.int32, shape, dim)


def reverse_bits(value, bits):
    return sum(((value // 2**j) % 2) * 2 ** (bits - 1 - j) for j in range(bits))


def kernel(
    nf,
    ns,
    tokens,
    weight_t,
    bias,
    rate_row,
    x,
    b_in,
    c_out,
    dy,
    out_x,
    out_b,
    out_c,
    out_w,
    gathered,
    raw_t,
    cum_t,
    step_t,
    block_t,
    cum_g,
    step_g,
    tail_g,
    lead_g,
    state_loc,
    grad_loc,
    xs_g,
    ds_g,
    entry,
    later,
    send_f,
    send_b,
    through,
    grad_b,
    grad_c,
    col_t,
    xt_t,
    xc_t,
    ent_t,
    total,
    rs_send,
    rs_recv,
    z_recv,
    ag_ssem,
    ag_rsem,
    f_ssem,
    f_rsem,
    b_ssem,
    b_rsem,
    rs_ssem,
    rs_rsem,
    z_ssem,
    z_rsem,
):
    f = lax.axis_index("fsdp")
    z = lax.axis_index("seq")
    length = tokens.shape[0]
    heads, rows = weight_t.shape
    groups = b_in.shape[1] // STATE
    per = heads // groups
    wide = x.shape[1] // groups
    size = wide // per
    bits = nf.bit_length() - 1

    def partner(j):
        return f + (1 - 2 * ((f // 2**j) % 2)) * 2**j

    barrier = pltpu.get_barrier_semaphore()
    for j in range(bits):
        pl.semaphore_signal(
            barrier, inc=1, device_id={"fsdp": partner(j)}, device_id_type=MESH
        )
    for d in range(1, ns):
        pl.semaphore_signal(
            barrier, inc=1, device_id={"seq": (z + d) % ns}, device_id_type=MESH
        )
    pl.semaphore_wait(barrier, bits + ns - 1)

    slot = reverse_bits(f, bits)
    gathered[slot] = weight_t[...]
    for i in range(bits):
        j = bits - 1 - i
        part = gathered.at[pl.ds((slot // 2**i) * 2**i, 2**i)]
        copy = pltpu.make_async_remote_copy(
            src_ref=part,
            dst_ref=part,
            send_sem=ag_ssem.at[i],
            recv_sem=ag_rsem.at[i],
            device_id={"fsdp": partner(j)},
            device_id_type=MESH,
        )
        copy.start()
        copy.wait()

    raw = jnp.broadcast_to(bias[...], (length, heads)).T
    rate = jnp.broadcast_to(rate_row[...], (length, heads)).T
    for s in range(nf):
        own = reverse_bits(s, bits)
        raw = raw + dot(gathered[s], tokens[:, own * rows : (own + 1) * rows], 1, 1)
    step = jnp.maximum(raw, 0.0) + jnp.log1p(jnp.exp(-jnp.abs(raw)))
    before = iota((length, length), 0) <= iota((length, length), 1)
    cum = dot(-rate * step, before.astype(F32), precision=HIGH)
    raw_t[...] = raw
    cum_t[...] = cum
    step_t[...] = step
    final = cum[:, length - 1 : length]
    block_t[...] = jnp.broadcast_to(jnp.exp(final), (heads, STATE))
    both = jnp.concatenate([cum, step], axis=0).T
    cum_c = both[:, :heads]
    step_c = both[:, heads:]
    tail_c = jnp.exp(cum_c[length - 1 : length] - cum_c)
    lead_c = jnp.exp(cum_c)
    for g in range(groups):
        span = slice(g * per, (g + 1) * per)
        cum_g[g] = cum_c[:, span]
        step_g[g] = step_c[:, span]
        tail_g[g] = tail_c[:, span]
        lead_g[g] = lead_c[:, span]

    spread_one = (iota((2 * per, wide), 0) % per == iota((2 * per, wide), 1) // size).astype(BF16)
    gather_one = (iota((per, wide), 0) == iota((per, wide), 1) // size).astype(BF16)

    def expand(value):
        return dot(halves(value, 1), spread_one)

    def head_sums(value):
        high = value.astype(BF16)
        low = (value - high.astype(F32)).astype(BF16)
        return dot(gather_one, high, 1, 1) + dot(gather_one, low, 1, 1)

    def span_of(g, width):
        return pl.ds(pl.multiple_of(g * width, width), width)

    @pl.when(z == 0)
    def _():
        entry[...] = jnp.zeros_like(entry)

    @pl.when(z == ns - 1)
    def _():
        later[...] = jnp.zeros_like(later)

    def forward_copy(g):
        return pltpu.make_async_remote_copy(
            src_ref=send_f.at[g],
            dst_ref=entry.at[g],
            send_sem=f_ssem.at[g],
            recv_sem=f_rsem.at[g],
            device_id={"seq": (z + 1) % ns},
            device_id_type=MESH,
        )

    def backward_copy(g):
        return pltpu.make_async_remote_copy(
            src_ref=send_b.at[g],
            dst_ref=later.at[g],
            send_sem=b_ssem.at[g],
            recv_sem=b_rsem.at[g],
            device_id={"seq": (z + ns - 1) % ns},
            device_id_type=MESH,
        )

    def local(g):
        xs = (x[:, span_of(g, wide)].astype(F32) * expand(step_g[g] * tail_g[g])).astype(BF16)
        ds = (dy[:, span_of(g, wide)].astype(F32) * expand(lead_g[g])).astype(BF16)
        xs_g[g] = xs
        ds_g[g] = ds
        state_loc[g] = dot(xs, b_in[:, span_of(g, STATE)], 0, 0)
        grad_loc[g] = dot(ds, c_out[:, span_of(g, STATE)], 0, 0)

    def decay_rows(g):
        return dot(spread_one, halves(block_t[span_of(g, per)], 0), 0, 0)

    def chain_f(g):
        @pl.when(z > 0)
        def _():
            forward_copy(g).wait_recv()

        @pl.when(z < ns - 1)
        def _():
            send_f[g] = (decay_rows(g) * entry[g].astype(F32) + state_loc[g]).astype(BF16)
            forward_copy(g).start()

    def chain_b(g):
        @pl.when(z < ns - 1)
        def _():
            backward_copy(g).wait_recv()

        @pl.when(z > 0)
        def _():
            send_b[g] = (decay_rows(g) * later[g].astype(F32) + grad_loc[g]).astype(BF16)
            backward_copy(g).start()

    def heavy(g):
        inputs = x[:, span_of(g, wide)]
        upstream = dy[:, span_of(g, wide)]
        b = b_in[:, span_of(g, STATE)]
        c = c_out[:, span_of(g, STATE)]
        meet = dot(b, c, 1, 1)
        upper = iota((length, length), 0) <= iota((length, length), 1)
        lanes = iota((length, 128), 1)
        cum_r = cum_t[span_of(g, per)]
        cum_l = cum_g[g]
        step_l = step_g[g]
        joint = jnp.zeros((length, length), F32)
        sums = []
        pieces = []
        for q in range(wide // 128):
            x_q = inputs[:, q * 128 : (q + 1) * 128]
            dy_q = upstream[:, q * 128 : (q + 1) * 128]
            weights = []
            masked = []
            for j in range(128 // size):
                k = q * (128 // size) + j
                mine = lanes // size == j
                pair = dot(jnp.where(mine, x_q, jnp.zeros_like(x_q)), dy_q, 1, 1)
                spread = cum_r[k : k + 1] - cum_l[:, k : k + 1]
                decay = jnp.exp(jnp.where(upper, spread, -1e30))
                weights.append((decay * meet).astype(BF16))
                masked.append(jnp.where(mine, dy_q, jnp.zeros_like(dy_q)))
                scaled = decay * pair * step_l[:, k : k + 1]
                joint = joint + scaled
                sums.append(jnp.sum(scaled * meet, axis=0, keepdims=True))
            pieces.append(
                dot(jnp.concatenate(weights, axis=1), jnp.concatenate(masked, axis=0))
            )
        passed = jnp.concatenate(pieces, axis=1)
        through[g] = passed
        col_t[span_of(g, per)] = jnp.concatenate(sums, axis=0)
        xt_t[span_of(g, per)] = head_sums(inputs.astype(F32) * passed)
        joint = joint.astype(BF16)
        grad_b[g] = dot(joint, c)
        grad_c[g] = dot(joint, b, 0, 0)

    def finish_f(g):
        c = c_out[:, span_of(g, STATE)]
        read = dot(c, entry[g], 1, 1)
        ent_t[span_of(g, per)] = head_sums(ds_g[g].astype(F32) * read)
        out_c[:, span_of(g, STATE)] = (grad_c[g] + dot(ds_g[g], entry[g])).astype(BF16)

    def finish_b(g):
        b = b_in[:, span_of(g, STATE)]
        carried = dot(b, later[g], 1, 1)
        xc_t[span_of(g, per)] = head_sums(x[:, span_of(g, wide)].astype(F32) * carried)
        inner = through[g] + expand(tail_g[g]) * carried
        out_x[:, span_of(g, wide)] = (expand(step_g[g]) * inner).astype(BF16)
        out_b[:, span_of(g, STATE)] = (grad_b[g] + dot(xs_g[g], later[g])).astype(BF16)

    def within(g):
        return jnp.logical_and(g >= 0, g < groups)

    def slot_step(tau, carry):
        gf = tau - z
        gb = tau - (ns - 1 - z)
        pl.when(tau < groups)(lambda: local(tau))
        pl.when(within(gf))(lambda: chain_f(gf))
        pl.when(within(gb))(lambda: chain_b(gb))
        pl.when(tau < groups)(lambda: heavy(tau))
        pl.when(within(gf))(lambda: finish_f(gf))
        pl.when(within(gb))(lambda: finish_b(gb))
        return carry

    lax.fori_loop(0, groups + ns - 1, slot_step, 0)

    crossing = jnp.concatenate(
        [
            dot(gather_one, (entry[g].astype(F32) * later[g].astype(F32)).astype(BF16))
            for g in range(groups)
        ],
        axis=0,
    )
    cum = cum_t[...]
    step = step_t[...]
    raw = raw_t[...]
    tail = jnp.exp(cum[:, length - 1 : length] - cum)
    xt = xt_t[...]
    tail_xc = tail * xc_t[...]
    leaving = step * tail_xc
    grad_cum = col_t[...] - step * xt + ent_t[...] - leaving
    closing = block_t[:, :1] * jnp.sum(crossing, axis=1, keepdims=True) + jnp.sum(
        leaving, axis=1, keepdims=True
    )
    after = (iota((length, length), 0) >= iota((length, length), 1)).astype(F32)
    grad_log = dot(grad_cum, after, precision=HIGH) + closing
    grad_raw = (xt + tail_xc - rate * grad_log) * jax.nn.sigmoid(raw)
    grad_raw = grad_raw.astype(BF16)

    base = 0
    count = nf
    for j in range(bits):
        bit = (f // 2**j) % 2
        half = count // 2
        if j == 0 and rows % 128 == 0:
            for i in range(half):
                own = 2 * i + (1 - bit)
                columns = pl.ds(pl.multiple_of(own * rows, 128), rows)
                rs_send[i_slot(i, bits)] = dot(grad_raw, tokens[:, columns]).astype(BF16)
        else:
            if j == 0:
                for s in range(nf):
                    own = reverse_bits(s, bits)
                    total[s] = dot(grad_raw, tokens[:, own * rows : (own + 1) * rows])
            rs_send[pl.ds(nf - count, half)] = total[
                pl.ds(base + (1 - bit) * half, half)
            ].astype(BF16)
        copy = pltpu.make_async_remote_copy(
            src_ref=rs_send.at[pl.ds(nf - count, half)],
            dst_ref=rs_recv.at[pl.ds(nf - count, half)],
            send_sem=rs_ssem.at[j],
            recv_sem=rs_rsem.at[j],
            device_id={"fsdp": partner(j)},
            device_id_type=MESH,
        )
        copy.start()
        if j == 0 and rows % 128 == 0:
            for i in range(half):
                own = 2 * i + bit
                columns = pl.ds(pl.multiple_of(own * rows, 128), rows)
                total[bit * half + i_slot(i, bits)] = dot(grad_raw, tokens[:, columns])
        copy.wait()
        base = base + bit * half
        total[pl.ds(base, half)] += rs_recv[pl.ds(nf - count, half)].astype(F32)
        count = half

    z_recv[z] = total[base].astype(BF16)
    copies = []
    for d in range(1, ns):
        copy = pltpu.make_async_remote_copy(
            src_ref=z_recv.at[z],
            dst_ref=z_recv.at[z],
            send_sem=z_ssem.at[d - 1],
            recv_sem=z_rsem.at[d - 1],
            device_id={"seq": (z + d) % ns},
            device_id_type=MESH,
        )
        copy.start()
        copies.append(copy)
    for copy in copies:
        copy.wait()
    summed = z_recv[0].astype(F32)
    for k in range(1, ns):
        summed = summed + z_recv[k].astype(F32)
    out_w[...] = summed

    @pl.when(z < ns - 1)
    def _():
        for g in range(groups):
            forward_copy(g).wait_send()

    @pl.when(z > 0)
    def _():
        for g in range(groups):
            backward_copy(g).wait_send()


def i_slot(i, bits):
    return reverse_bits(i, bits - 1)


def body(
    layer_input, dt_weight, dt_bias, decay_rate, ssm_input, in_basis, out_basis, out_cotangent
):
    nf, ns = lax.axis_size("fsdp"), lax.axis_size("seq")
    length = layer_input.shape[1]
    rows, heads = dt_weight.shape
    groups = in_basis.shape[2] // STATE
    per = heads // groups
    full = ssm_input.shape[2]
    wide = full // groups
    bits = nf.bit_length() - 1
    tall = (groups, wide, STATE)
    dma = pltpu.SemaphoreType.DMA
    v = pltpu.VMEM
    scratch = [
        v((nf, heads, rows), BF16),
        v((heads, length), F32),
        v((heads, length), F32),
        v((heads, length), F32),
        v((heads, STATE), F32),
        v((groups, length, per), F32),
        v((groups, length, per), F32),
        v((groups, length, per), F32),
        v((groups, length, per), F32),
        v(tall, F32),
        v(tall, F32),
        v((groups, length, wide), BF16),
        v((groups, length, wide), BF16),
        v(tall, BF16),
        v(tall, BF16),
        v(tall, BF16),
        v(tall, BF16),
        v((groups, length, wide), F32),
        v((groups, length, STATE), F32),
        v((groups, length, STATE), F32),
        v((heads, length), F32),
        v((heads, length), F32),
        v((heads, length), F32),
        v((heads, length), F32),
        v((nf, heads, rows), F32),
        v((nf, heads, rows), BF16),
        v((nf, heads, rows), BF16),
        v((ns, heads, rows), BF16),
        dma((bits,)),
        dma((bits,)),
        dma((groups,)),
        dma((groups,)),
        dma((groups,)),
        dma((groups,)),
        dma((bits,)),
        dma((bits,)),
        dma((ns - 1,)),
        dma((ns - 1,)),
    ]
    out_x, out_b, out_c, out_w = pl.pallas_call(
        functools.partial(kernel, nf, ns),
        out_shape=(
            jax.ShapeDtypeStruct((length, full), BF16),
            jax.ShapeDtypeStruct((length, groups * STATE), BF16),
            jax.ShapeDtypeStruct((length, groups * STATE), BF16),
            jax.ShapeDtypeStruct((heads, rows), F32),
        ),
        in_specs=[pl.BlockSpec(memory_space=pltpu.VMEM)] * 8,
        out_specs=[pl.BlockSpec(memory_space=pltpu.VMEM)] * 4,
        scratch_shapes=scratch,
        compiler_params=pltpu.CompilerParams(
            collective_id=0, has_side_effects=True, vmem_limit_bytes=60 * 1024 * 1024
        ),
    )(
        layer_input[0],
        dt_weight.T,
        dt_bias[None],
        decay_rate[None],
        ssm_input[0],
        in_basis[0],
        out_basis[0],
        out_cotangent[0],
    )
    return (out_x[None], out_b[None], out_c[None], out_w.T)


def solution(mesh):
    blocks = P("fsdp", "seq", None)
    rows = P("fsdp", None)
    return jax.shard_map(
        body,
        mesh=mesh,
        in_specs=(blocks, rows, P(), P(), blocks, blocks, blocks, blocks),
        out_specs=(blocks, blocks, blocks, rows),
        check_vma=False,
    )
```

time: 258 us -> 64.9 us (0.25)
  waiting for transfers between devices: 147 us -> 0 us
  Pallas kernels: 0 us -> 59.5 us
  blocking collectives: 31.8 us -> 0 us
  matrix products: 26 us -> 0 us
  other arithmetic: 18.5 us -> 0 us
  local copies, waits for them, and re-layouts: 19.2 us -> 4.48 us
  between operations: 14.3 us -> 0.65 us
    all_gather x2 -> x0, waiting for transfers between devices: 82.4 us -> none  [the longest x1 67.5 us: prefix(): pieces = jax.tree.map(lambda part: lax.all_gather(part, axis), value)]
    pallas_call x0 -> x1, Pallas kernels: none -> 59.5 us  [body(): pl.pallas_call(functools.partial(kernel, nf, ns), out_shape=(jax.ShapeDty...]
    psum x1 -> x0, waiting for transfers between devices: 33.7 us -> none  [body(): grad_weight = lax.psum(partial_rows, 'seq')]
    all_gather x3 -> x0, blocking collectives: 31.8 us -> none  [the longest x1 11.8 us: body(): lax.all_gather(dt_weight, 'fsdp', axis=0, tiled=True)]
    reduce_scatter x1 -> x0, waiting for transfers between devices: 30.4 us -> none  [body(): lax.psum_scatter(jnp.dot(columns.T, grad_raw, precision=HIGH), 'fsdp', sc...]
    dot_general x12 -> x0, matrix products: 26 us -> none  [the longest x1 5.36 us: body(): state_read = jnp.einsum('tgkp,gkpn->tgkn', upstream, entry, precision=HIGH)]
    select_n x7 -> x0, other arithmetic: 9.92 us -> none  [the longest x4 5.48 us: entering_step(): return jax.tree.map(lambda a, b: jnp.where(reached, a, b), new, before)]
    rev x5 -> x0, local copies, waits for them, and re-layouts: 5.51 us -> none  [the longest x2 5.21 us: prefix(): pieces = jax.tree.map(lambda part: part[::-1], pieces)]
  transfers between devices with their start and end apart: 4 -> 0, of which waited for: 4 -> 0; matrix products, arithmetic and copies ran while one was open for 12% -> 0% of each run, Pallas kernels for 0% -> 0%
where the time goes in v1:
time: 64.9 us; the launch traced here: 64.7 us
  Pallas kernels  59.5 us (92%)
  local copies, waits for them, and re-layouts  4.48 us (7%)
  between operations  0.65 us (1%)
    pallas_call x1, Pallas kernels, body(): pl.pallas_call(functools.partial(kernel, nf, ns), out_shape=(jax.ShapeDty...  59.5 us
    unnamed x10, local copies, waits for them, and re-layouts  4.48 us

profile of v1, /device:TPU:0, one launch (start us, length us, event | category | flops | bytes accessed | tf_op | source)
XLA Modules:
  0.0 64.7 jit_solution(4244031424989479806)
XLA Ops:
  0.6 59.5 %shard_map.111 = (bf16[128,2048]{1,0:T(8,128)(2,1)}, bf16[128,512]{1,0:T(8,128)(2,1)}, bf16[128,512]{1,0:T(8,128)(2,1)}, f32[64,512]{1,0:T(8,128)}) custom-call(bf16[128,4096]{1,0:T(8,128)(2,1)} %bitcast.12, bf16[64,512]{1,0:T(8,128)(2,1)} %bitcast.21, f32[1,64]{1,0:T(1,128)} %bitcast.22, f32[1,64]{1,0:T(1,128)} %bitcast.23, bf16[128,2048]{1,0:T(8,128)(2,1)} %bitcast.14, ...), custom_call_target="tpu_custom_call" | custom-call | tf_op jit(solution)/shard_map/pallas_call | solution.py:449
  60.2 0.0 copy-start.2
  60.2 1.9 %copy.16 = bf16[1,128,2048]{2,1,0:T(8,128)(2,1)} copy(bf16[1,128,2048]{2,1,0:T(8,128)(2,1)} %bitcast.13) | data formatting | bytes 1048576
  62.1 0.0 copy-done.2
  62.1 0.0 copy-start.1
  62.1 0.7 %copy.17 = bf16[1,128,512]{2,1,0:T(8,128)(2,1)} copy(bf16[1,128,512]{2,1,0:T(8,128)(2,1)S(1)} %bitcast.20) | data formatting | bytes 262144
  62.8 0.3 copy-done.1
  63.1 0.0 copy-start
  63.1 0.7 %copy.18 = bf16[1,128,512]{2,1,0:T(8,128)(2,1)} copy(bf16[1,128,512]{2,1,0:T(8,128)(2,1)S(1)} %bitcast.19) | data formatting | bytes 262144
  63.7 0.3 copy-done
  64.0 0.7 %copy.19 = f32[512,64]{0,1:T(8,128)} copy(f32[512,64]{0,1:T(8,128)S(1)} %bitcast.18) | data formatting | bytes 262144
Async XLA Ops:
  60.2 1.9 %copy-start.2 = (bf16[128,512]{1,0:T(8,128)(2,1)S(1)}, bf16[128,512]{1,0:T(8,128)(2,1)}, u32[]{:S(2)}) copy-start(bf16[128,512]{1,0:T(8,128)(2,1)} %get-tuple-element.9) | copy-start | bytes 393220
  62.1 1.0 %copy-start.1 = (bf16[128,512]{1,0:T(8,128)(2,1)S(1)}, bf16[128,512]{1,0:T(8,128)(2,1)}, u32[]{:S(2)}) copy-start(bf16[128,512]{1,0:T(8,128)(2,1)} %get-tuple-element.10) | copy-start | bytes 393220
  63.1 1.0 %copy-start = (f32[64,512]{1,0:T(8,128)S(1)}, f32[64,512]{1,0:T(8,128)}, u32[]{:S(2)}) copy-start(f32[64,512]{1,0:T(8,128)} %get-tuple-element.11) | copy-start | bytes 393220

commit v2 on v1

--- a/solution.py
+++ b/solution.py
@@ -30,17 +30,22 @@
     return lax.broadcasted_iota(jnp.int32, shape, dim)
 
 
-def reverse_bits(value, bits):
-    return sum(((value // 2**j) % 2) * 2 ** (bits - 1 - j) for j in range(bits))
-
-
 def kernel(
     nf,
     ns,
-    tokens,
+    tokens_hbm,
     weight_t,
     bias,
     rate_row,
+    x_hbm,
+    b_hbm,
+    c_hbm,
+    dy_hbm,
+    x_out,
+    b_out,
+    c_out_hbm,
+    out_w,
+    tokens,
     x,
     b_in,
     c_out,
@@ -48,7 +53,8 @@
     out_x,
     out_b,
     out_c,
-    out_w,
+    in_sem,
+    out_sem,
     gathered,
     raw_t,
     cum_t,
@@ -97,6 +103,26 @@
     wide = x.shape[1] // groups
     size = wide // per
     bits = nf.bit_length() - 1
+    part_heads = heads // 2
+    chunk = wide // 2
+    loads = [
+        pltpu.make_async_copy(source, target, in_sem.at[n])
+        for n, (source, target) in enumerate(
+            (
+                (tokens_hbm, tokens),
+                (x_hbm, x),
+                (dy_hbm, dy),
+                (b_hbm, b_in),
+                (c_hbm, c_out),
+            )
+        )
+    ]
+    for load in loads:
+        load.start()
+    orders = (list(reversed(range(bits))), list(range(1, bits)) + [0])
+
+    def slot_of(index, order):
+        return sum(((index // 2**b) % 2) * 2**i for i, b in enumerate(order))
 
     def partner(j):
         return f + (1 - 2 * ((f // 2**j) % 2)) * 2**j
@@ -112,27 +138,36 @@
         )
     pl.semaphore_wait(barrier, bits + ns - 1)
 
-    slot = reverse_bits(f, bits)
-    gathered[slot] = weight_t[...]
+    slots = [slot_of(f, order) for order in orders]
+    for h in range(2):
+        gathered[h, slots[h]] = weight_t[h * part_heads : (h + 1) * part_heads]
     for i in range(bits):
-        j = bits - 1 - i
-        part = gathered.at[pl.ds((slot // 2**i) * 2**i, 2**i)]
-        copy = pltpu.make_async_remote_copy(
-            src_ref=part,
-            dst_ref=part,
-            send_sem=ag_ssem.at[i],
-            recv_sem=ag_rsem.at[i],
-            device_id={"fsdp": partner(j)},
-            device_id_type=MESH,
-        )
-        copy.start()
-        copy.wait()
+        copies = []
+        for h in range(2):
+            part = gathered.at[h, pl.ds((slots[h] // 2**i) * 2**i, 2**i)]
+            copy = pltpu.make_async_remote_copy(
+                src_ref=part,
+                dst_ref=part,
+                send_sem=ag_ssem.at[h, i],
+                recv_sem=ag_rsem.at[h, i],
+                device_id={"fsdp": partner(orders[h][i])},
+                device_id_type=MESH,
+            )
+            copy.start()
+            copies.append(copy)
+        if i == bits - 1:
+            for load in loads:
+                load.wait()
+        for copy in copies:
+            copy.wait()
 
     raw = jnp.broadcast_to(bias[...], (length, heads)).T
     rate = jnp.broadcast_to(rate_row[...], (length, heads)).T
-    for s in range(nf):
-        own = reverse_bits(s, bits)
-        raw = raw + dot(gathered[s], tokens[:, own * rows : (own + 1) * rows], 1, 1)
+    for own in range(nf):
+        weight = jnp.concatenate(
+            [gathered[h, slot_of(own, orders[h])] for h in range(2)], axis=0
+        )
+        raw = raw + dot(weight, tokens[:, own * rows : (own + 1) * rows], 1, 1)
     step = jnp.maximum(raw, 0.0) + jnp.log1p(jnp.exp(-jnp.abs(raw)))
     before = iota((length, length), 0) <= iota((length, length), 1)
     cum = dot(-rate * step, before.astype(F32), precision=HIGH)
@@ -175,10 +210,17 @@
     def _():
         later[...] = jnp.zeros_like(later)
 
+    spread_half = (
+        iota((per, chunk), 0) % (per // 2) == iota((per, chunk), 1) // size
+    ).astype(BF16)
+
+    def piece(g):
+        return g // 2, pl.ds(pl.multiple_of((g % 2) * chunk, chunk), chunk)
+
     def forward_copy(g):
         return pltpu.make_async_remote_copy(
-            src_ref=send_f.at[g],
-            dst_ref=entry.at[g],
+            src_ref=send_f.at[piece(g)],
+            dst_ref=entry.at[piece(g)],
             send_sem=f_ssem.at[g],
             recv_sem=f_rsem.at[g],
             device_id={"seq": (z + 1) % ns},
@@ -187,8 +229,8 @@
 
     def backward_copy(g):
         return pltpu.make_async_remote_copy(
-            src_ref=send_b.at[g],
-            dst_ref=later.at[g],
+            src_ref=send_b.at[piece(g)],
+            dst_ref=later.at[piece(g)],
             send_sem=b_ssem.at[g],
             recv_sem=b_rsem.at[g],
             device_id={"seq": (z + ns - 1) % ns},
@@ -204,7 +246,7 @@
         grad_loc[g] = dot(ds, c_out[:, span_of(g, STATE)], 0, 0)
 
     def decay_rows(g):
-        return dot(spread_one, halves(block_t[span_of(g, per)], 0), 0, 0)
+        return dot(spread_half, halves(block_t[span_of(g, per // 2)], 0), 0, 0)
 
     def chain_f(g):
         @pl.when(z > 0)
@@ -213,7 +255,8 @@
 
         @pl.when(z < ns - 1)
         def _():
-            send_f[g] = (decay_rows(g) * entry[g].astype(F32) + state_loc[g]).astype(BF16)
+            p = piece(g)
+            send_f[p] = (decay_rows(g) * entry[p].astype(F32) + state_loc[p]).astype(BF16)
             forward_copy(g).start()
 
     def chain_b(g):
@@ -223,7 +266,8 @@
 
         @pl.when(z > 0)
         def _():
-            send_b[g] = (decay_rows(g) * later[g].astype(F32) + grad_loc[g]).astype(BF16)
+            p = piece(g)
+            send_b[p] = (decay_rows(g) * later[p].astype(F32) + grad_loc[p]).astype(BF16)
             backward_copy(g).start()
 
     def heavy(g):
@@ -288,14 +332,24 @@
         gf = tau - z
         gb = tau - (ns - 1 - z)
         pl.when(tau < groups)(lambda: local(tau))
-        pl.when(within(gf))(lambda: chain_f(gf))
-        pl.when(within(gb))(lambda: chain_b(gb))
+        pl.when(within(gf))(lambda: chain_f(2 * gf))
+        pl.when(within(gb))(lambda: chain_b(2 * gb))
         pl.when(tau < groups)(lambda: heavy(tau))
+        pl.when(within(gf))(lambda: chain_f(2 * gf + 1))
+        pl.when(within(gb))(lambda: chain_b(2 * gb + 1))
         pl.when(within(gf))(lambda: finish_f(gf))
         pl.when(within(gb))(lambda: finish_b(gb))
         return carry
 
     lax.fori_loop(0, groups + ns - 1, slot_step, 0)
+    stores = [
+        pltpu.make_async_copy(source, target, out_sem.at[n])
+        for n, (source, target) in enumerate(
+            ((out_x, x_out), (out_b, b_out), (out_c, c_out_hbm))
+        )
+    ]
+    for store in stores:
+        store.start()
 
     crossing = jnp.concatenate(
         [
@@ -320,44 +374,60 @@
     grad_raw = (xt + tail_xc - rate * grad_log) * jax.nn.sigmoid(raw)
     grad_raw = grad_raw.astype(BF16)
 
-    base = 0
+    bases = [0, 0]
     count = nf
+    early = rows % 128 == 0
+
+    def product(own, target, place, offset):
+        columns = pl.ds(pl.multiple_of(own * rows, 128), rows) if early else slice(
+            own * rows, (own + 1) * rows
+        )
+        block = dot(grad_raw, tokens[:, columns])
+        for h in range(2):
+            target[h, offset + place[h]] = block[
+                h * part_heads : (h + 1) * part_heads
+            ].astype(target.dtype)
+
     for j in range(bits):
-        bit = (f // 2**j) % 2
         half = count // 2
-        if j == 0 and rows % 128 == 0:
+        sent = pl.ds(nf - count, half)
+        if j == 0 and early:
+            bit = f % 2
             for i in range(half):
-                own = 2 * i + (1 - bit)
-                columns = pl.ds(pl.multiple_of(own * rows, 128), rows)
-                rs_send[i_slot(i, bits)] = dot(grad_raw, tokens[:, columns]).astype(BF16)
-        else:
-            if j == 0:
-                for s in range(nf):
-                    own = reverse_bits(s, bits)
-                    total[s] = dot(grad_raw, tokens[:, own * rows : (own + 1) * rows])
-            rs_send[pl.ds(nf - count, half)] = total[
-                pl.ds(base + (1 - bit) * half, half)
-            ].astype(BF16)
-        copy = pltpu.make_async_remote_copy(
-            src_ref=rs_send.at[pl.ds(nf - count, half)],
-            dst_ref=rs_recv.at[pl.ds(nf - count, half)],
-            send_sem=rs_ssem.at[j],
-            recv_sem=rs_rsem.at[j],
-            device_id={"fsdp": partner(j)},
-            device_id_type=MESH,
-        )
-        copy.start()
-        if j == 0 and rows % 128 == 0:
+                place = [slot_of(2 * i, order) for order in orders]
+                product(2 * i + (1 - bit), rs_send, place, 0)
+        elif j == 0:
+            for own in range(nf):
+                product(own, total, [slot_of(own, order) for order in orders], 0)
+        copies = []
+        for h in range(2):
+            b = orders[h][bits - 1 - j]
+            bit_h = (f // 2**b) % 2
+            if j > 0 or not early:
+                rs_send[h, sent] = total[
+                    h, pl.ds(bases[h] + (1 - bit_h) * half, half)
+                ].astype(BF16)
+            copy = pltpu.make_async_remote_copy(
+                src_ref=rs_send.at[h, sent],
+                dst_ref=rs_recv.at[h, sent],
+                send_sem=rs_ssem.at[h, j],
+                recv_sem=rs_rsem.at[h, j],
+                device_id={"fsdp": partner(b)},
+                device_id_type=MESH,
+            )
+            copy.start()
+            copies.append(copy)
+            bases[h] = bases[h] + bit_h * half
+        if j == 0 and early:
             for i in range(half):
-                own = 2 * i + bit
-                columns = pl.ds(pl.multiple_of(own * rows, 128), rows)
-                total[bit * half + i_slot(i, bits)] = dot(grad_raw, tokens[:, columns])
-        copy.wait()
-        base = base + bit * half
-        total[pl.ds(base, half)] += rs_recv[pl.ds(nf - count, half)].astype(F32)
+                place = [slot_of(2 * i, order) for order in orders]
+                product(2 * i + bit, total, place, bit * half)
+        for h in range(2):
+            copies[h].wait()
+            total[h, pl.ds(bases[h], half)] += rs_recv[h, sent].astype(F32)
         count = half
 
-    z_recv[z] = total[base].astype(BF16)
+    z_recv[z] = jnp.concatenate([total[h, bases[h]] for h in range(2)], axis=0).astype(BF16)
     copies = []
     for d in range(1, ns):
         copy = pltpu.make_async_remote_copy(
@@ -379,17 +449,16 @@
 
     @pl.when(z < ns - 1)
     def _():
-        for g in range(groups):
+        for g in range(2 * groups):
             forward_copy(g).wait_send()
 
     @pl.when(z > 0)
     def _():
-        for g in range(groups):
+        for g in range(2 * groups):
             backward_copy(g).wait_send()
 
-
-def i_slot(i, bits):
-    return reverse_bits(i, bits - 1)
+    for store in stores:
+        store.wait()
 
 
 def body(
@@ -407,7 +476,17 @@
     dma = pltpu.SemaphoreType.DMA
     v = pltpu.VMEM
     scratch = [
-        v((nf, heads, rows), BF16),
+        v((length, layer_input.shape[2]), BF16),
+        v((length, full), BF16),
+        v((length, groups * STATE), BF16),
+        v((length, groups * STATE), BF16),
+        v((length, full), BF16),
+        v((length, full), BF16),
+        v((length, groups * STATE), BF16),
+        v((length, groups * STATE), BF16),
+        dma((5,)),
+        dma((3,)),
+        v((2, nf, heads // 2, rows), BF16),
         v((heads, length), F32),
         v((heads, length), F32),
         v((heads, length), F32),
@@ -431,21 +510,23 @@
         v((heads, length), F32),
         v((heads, length), F32),
         v((heads, length), F32),
-        v((nf, heads, rows), F32),
-        v((nf, heads, rows), BF16),
-        v((nf, heads, rows), BF16),
+        v((2, nf, heads // 2, rows), F32),
+        v((2, nf, heads // 2, rows), BF16),
+        v((2, nf, heads // 2, rows), BF16),
         v((ns, heads, rows), BF16),
-        dma((bits,)),
-        dma((bits,)),
-        dma((groups,)),
-        dma((groups,)),
-        dma((groups,)),
-        dma((groups,)),
-        dma((bits,)),
-        dma((bits,)),
+        dma((2, bits)),
+        dma((2, bits)),
+        dma((2 * groups,)),
+        dma((2 * groups,)),
+        dma((2 * groups,)),
+        dma((2 * groups,)),
+        dma((2, bits)),
+        dma((2, bits)),
         dma((ns - 1,)),
         dma((ns - 1,)),
     ]
+    anywhere = pl.BlockSpec(memory_space=pl.ANY)
+    inside = pl.BlockSpec(memory_space=pltpu.VMEM)
     out_x, out_b, out_c, out_w = pl.pallas_call(
         functools.partial(kernel, nf, ns),
         out_shape=(
@@ -454,8 +535,8 @@
             jax.ShapeDtypeStruct((length, groups * STATE), BF16),
             jax.ShapeDtypeStruct((heads, rows), F32),
         ),
-        in_specs=[pl.BlockSpec(memory_space=pltpu.VMEM)] * 8,
-        out_specs=[pl.BlockSpec(memory_space=pltpu.VMEM)] * 4,
+        in_specs=[anywhere] + [inside] * 3 + [anywhere] * 4,
+        out_specs=[anywhere] * 3 + [inside],
         scratch_shapes=scratch,
         compiler_params=pltpu.CompilerParams(
             collective_id=0, has_side_effects=True, vmem_limit_bytes=60 * 1024 * 1024

time: 64.9 us -> 59.4 us (0.915)
  Pallas kernels: 59.5 us -> 54.1 us
    pallas_call x1, Pallas kernels: 59.5 us -> 54.1 us  [body(): pl.pallas_call(functools.partial(kernel, nf, ns), out_shape=(jax.ShapeDty...]
where the time goes in v2:
time: 59.4 us; the launch traced here: 59.2 us
  Pallas kernels  54.1 us (91%)
  local copies, waits for them, and re-layouts  4.48 us (8%)
  between operations  0.65 us (1%)
    pallas_call x1, Pallas kernels, body(): pl.pallas_call(functools.partial(kernel, nf, ns), out_shape=(jax.ShapeDty...  54.1 us
    unnamed x10, local copies, waits for them, and re-layouts  4.48 us

profile of v2, /device:TPU:0, one launch (start us, length us, event | category | flops | bytes accessed | tf_op | source)
XLA Modules:
  0.0 59.2 jit_solution(11027189856904310001)
XLA Ops:
  0.6 54.1 %shard_map.111 = (bf16[128,2048]{1,0:T(8,128)(2,1)}, bf16[128,512]{1,0:T(8,128)(2,1)}, bf16[128,512]{1,0:T(8,128)(2,1)}, f32[64,512]{1,0:T(8,128)}) custom-call(bf16[128,4096]{1,0:T(8,128)(2,1)} %bitcast.12, bf16[64,512]{1,0:T(8,128)(2,1)} %bitcast.21, f32[1,64]{1,0:T(1,128)} %bitcast.22, f32[1,64]{1,0:T(1,128)} %bitcast.23, bf16[128,2048]{1,0:T(8,128)(2,1)} %bitcast.14, ...), custom_call_target="tpu_custom_call" | custom-call | tf_op jit(solution)/shard_map/pallas_call | solution.py:530
  54.7 0.0 copy-start.2
  54.7 1.9 %copy.16 = bf16[1,128,2048]{2,1,0:T(8,128)(2,1)} copy(bf16[1,128,2048]{2,1,0:T(8,128)(2,1)} %bitcast.13) | data formatting | bytes 1048576
  56.7 0.0 copy-done.2
  56.7 0.0 copy-start.1
  56.7 0.7 %copy.17 = bf16[1,128,512]{2,1,0:T(8,128)(2,1)} copy(bf16[1,128,512]{2,1,0:T(8,128)(2,1)S(1)} %bitcast.20) | data formatting | bytes 262144
  57.3 0.3 copy-done.1
  57.6 0.0 copy-start
  57.6 0.7 %copy.18 = bf16[1,128,512]{2,1,0:T(8,128)(2,1)} copy(bf16[1,128,512]{2,1,0:T(8,128)(2,1)S(1)} %bitcast.19) | data formatting | bytes 262144
  58.3 0.3 copy-done
  58.6 0.7 %copy.19 = f32[512,64]{0,1:T(8,128)} copy(f32[512,64]{0,1:T(8,128)S(1)} %bitcast.18) | data formatting | bytes 262144
Async XLA Ops:
  54.7 1.9 %copy-start.2 = (bf16[128,512]{1,0:T(8,128)(2,1)S(1)}, bf16[128,512]{1,0:T(8,128)(2,1)}, u32[]{:S(2)}) copy-start(bf16[128,512]{1,0:T(8,128)(2,1)} %get-tuple-element.9) | copy-start | bytes 393220
  56.7 1.0 %copy-start.1 = (bf16[128,512]{1,0:T(8,128)(2,1)S(1)}, bf16[128,512]{1,0:T(8,128)(2,1)}, u32[]{:S(2)}) copy-start(bf16[128,512]{1,0:T(8,128)(2,1)} %get-tuple-element.10) | copy-start | bytes 393220
  57.6 1.0 %copy-start = (f32[64,512]{1,0:T(8,128)S(1)}, f32[64,512]{1,0:T(8,128)}, u32[]{:S(2)}) copy-start(f32[64,512]{1,0:T(8,128)} %get-tuple-element.11) | copy-start | bytes 393220
